TPU v7x, 512 devices: a whole 4x8x8 slice. The times are simulated.
512 devices in a mesh: row: 16 (over y, core), col: 32 (over x, z).
Axes of the slice: x: 4, y: 8, z: 8, core: 2. Of those that a mesh axis runs over, the one named last changes fastest.
Arguments:
- lhat: float32 [4096, 256, 256], P(('row', 'col')), may hold values from -0.375 to 0.375
- ainv_anc: float32 [4096, 256, 256], P(('row', 'col')), may hold values from -1.25 to 1.25
- diag_inv: float32 [32, 256, 256], P('col', 'row'), may hold values from -0.6 to 2, as said below
- targets: int32 [4096, 1], P(('row', 'col')), may hold values from 0 to 31
Outputs:
- diag_blocks: float32 [32, 256, 256], P('col', 'row')
Inputs may be any that keep to these rules, and one draw needn't show every extreme that they name: `diag_inv`: each block is lower triangular with its diagonal entries between 0.5 and 2.
All inputs are finite; a program needn't handle non-finite values.
Results may differ from a plain program's by a relative error of at most 0.0003.
Values sent between devices are 32-bit elements; how exact they have to be, the bound alone decides.
No kernel may reach another device: no remote copies, remote signals or barrier semaphores. Data moves between devices by JAX's collectives and lax.ppermute only.
A program may use at most 64 MiB of HBM per device.

v0:
```python
import jax
import jax.numpy as jnp
from jax import lax
from jax.experimental import pallas as pl
from jax.experimental.pallas import tpu as pltpu
from jax.sharding import PartitionSpec as P


NY, NC, NX, NZ = 8, 2, 4, 8
BOTH = ("row", "col")


def flat(y, c, x, z):
    return ((y * NC + c) * NX + x) * NZ + z


def every():
    return [(y, c, x, z) for y in range(NY) for c in range(NC) for x in range(NX) for z in range(NZ)]


PLANES = [[flat(y, 0, x, z) for x in range(NX) for z in range(NZ)] for y in range(NY)] + [
    [flat(y, 1, x, z) for x in range(NX) for y in range(NY)] for z in range(NZ)
]
SHIFTS = (4, 3, 5, 2, 6, 1, 7)
EARLY = 4


def along(shift):
    return [
        (flat(y, c, x, z), flat((y + shift) % NY, 0, x, z) if c == 0 else flat(y, 1, x, (z + shift) % NZ))
        for y, c, x, z in every()
    ]


PARTNER = [(flat(y, c, x, z), flat(y, 1 - c, x, z)) for y, c, x, z in every()]
TO_ODD = [(flat(y, 0, x, z), flat(y, 1, x, z)) for y, c, x, z in every() if c == 0]
FAR = NY // 2
TURN = [(flat(y, 1, x, z), flat(z, 1, x, (y + FAR) % NZ)) for y, c, x, z in every() if c == 1]


def split(a):
    high = a.astype(jnp.bfloat16)
    return high, (a - high.astype(jnp.float32)).astype(jnp.bfloat16)


def times(turned, b):
    ah, al = turned
    bh, bl = split(b)
    left = jnp.concatenate([ah, ah, al], axis=1)
    right = jnp.concatenate([bh, bl, bh], axis=0)
    return jnp.dot(left, right, preferred_element_type=jnp.float32)


def tile_of(ids_ref, rows_ref, index):
    share, width = rows_ref.shape[1:]
    first = share * index + 1
    row = lax.broadcasted_iota(jnp.int32, (share, width), 0)
    lane = lax.broadcasted_iota(jnp.int32, (share, width), 1)
    tile = jnp.where(lane < first + row, rows_ref[0], 0.0)
    for s in range(ids_ref.shape[0]):
        tile = jnp.where((row == 0) & (lane == first + s), ids_ref[s].astype(jnp.float32), tile)
    return tile


def sent_kernel(
    ids_hbm, left_ref, right_ref, rows_hbm, sent_ref, own_ref, held_ref, tile_ref, ids_ref, rows_ref, scratch_ref, small, sems
):
    slots = left_ref.shape[0]
    share, width = rows_ref.shape[1:]
    few = (
        pltpu.make_async_copy(ids_hbm, ids_ref, small.at[0]),
        pltpu.make_async_copy(rows_hbm, rows_ref, small.at[1]),
    )
    for copy in few:
        copy.start()
    copies = []
    for s in range(slots):
        pair = (
            pltpu.make_async_copy(left_ref.at[s], scratch_ref.at[s], sems.at[0, s]),
            pltpu.make_async_copy(right_ref.at[s], held_ref.at[s], sems.at[1, s]),
        )
        for copy in pair:
            copy.start()
        copies.append(pair)
    index = lax.axis_index("row")
    core = index % NC
    for s in range(slots):
        for copy in copies[s]:
            copy.wait()
        parts = []
        for i, part in enumerate(split(scratch_ref[s])):
            part = part.T.reshape(NY, NC, share, width)
            even, odd = part[:, 0].reshape(NY * share, width), part[:, 1].reshape(NY * share, width)
            own_ref[i, s] = jnp.where(core == 0, even, odd)
            parts.append(jnp.where(core == 0, odd, even))
        product = times(parts, held_ref[s])
        sent_ref[:, s * share : (s + 1) * share] = product.reshape(NY, share, width)
    for copy in few:
        copy.wait()
    tile = tile_of(ids_ref, rows_ref, index)
    tile_ref[...] = tile
    for d in range(NY):
        sent_ref[d, slots * share :] = tile


def kept_kernel(own_ref, held_ref, tile_ref, kept_ref):
    slots = held_ref.shape[0]
    share, width = tile_ref.shape
    for s in range(slots):
        product = times((own_ref[0, s], own_ref[1, s]), held_ref[s])
        kept_ref[:, s * share : (s + 1) * share] = product.reshape(NY, share, width)
    for d in range(NY):
        kept_ref[d, slots * share :] = tile_ref[...]


def place_kernel(kept_ref, arrived_ref, *out_refs):
    index = lax.axis_index("row")
    me = jnp.where(index % NC == 0, index // NC, lax.axis_index("col") % NZ)
    for shift, out_ref in zip((0, *SHIFTS), out_refs):
        out_ref[0] = kept_ref[(me + shift) % NY]
        out_ref[1] = arrived_ref[(me + shift) % NY]


def add_blocks(shifts, got_refs, ids_refs, sems, out_ref, factor_ref):
    share = out_ref.shape[1]
    slots = got_refs[0].shape[1] // share - 1
    base = slots * share
    copies = [
        pltpu.make_async_copy(got_ref.at[:, base : base + 1], ids_ref, sems.at[i])
        for i, (got_ref, ids_ref) in enumerate(zip(got_refs, ids_refs))
    ]
    for copy in copies:
        copy.start()
    index = lax.axis_index("row")
    core = index % NC
    flip = core * FAR

    def first_of(shift, half):
        source_core = core if half == 0 else 1 - core
        return share * (jnp.where(core == 0, (index // NC + NY - shift) % NY, index // NC) * NC + source_core) + 1

    for shift, got_ref in zip(shifts, got_refs):
        source = (index // NC + NY - shift) % NY
        for half in range(NC):
            tile = got_ref[half, base:]
            row = lax.broadcasted_iota(jnp.int32, tile.shape, 0)
            lane = lax.broadcasted_iota(jnp.int32, tile.shape, 1)
            at = pl.multiple_of((source * NC + half) * share, share)
            factor_ref[pl.ds(at, share)] = jnp.where(lane < first_of(shift, half) + row, tile, 0.0)
    for copy in copies:
        copy.wait()
    for shift, got_ref, ids_ref in zip(shifts, got_refs, ids_refs):
        for half in range(NC):
            first = first_of(shift, half)
            for s in range(slots):
                k = ids_ref[half, 0, first + s].astype(jnp.int32)
                out_ref[k ^ flip] += got_ref[half, s * share : (s + 1) * share]


def early_kernel(*refs):
    n = EARLY + 1
    got_refs, (out_ref, factor_ref), ids_refs, sems = refs[:n], refs[n : n + 2], refs[n + 2 : -1], refs[-1]
    out_ref[...] = jnp.zeros_like(out_ref)
    factor_ref[...] = jnp.zeros_like(factor_ref)
    add_blocks((0, *SHIFTS[:EARLY]), got_refs, ids_refs, sems, out_ref, factor_ref)


def late_kernel(sum_ref, rows_ref, *refs):
    n = len(SHIFTS) - EARLY
    got_refs, (out_ref, factor_ref), ids_refs, sems = refs[:n], refs[n : n + 2], refs[n + 2 : -1], refs[-1]
    out_ref[...] = sum_ref[...]
    factor_ref[...] = rows_ref[...]
    add_blocks(SHIFTS[EARLY:], got_refs, ids_refs, sems, out_ref, factor_ref)


def gram_kernel(factor_ref, own_ref, other_ref, whole_ref):
    whole_ref[...] = times(split(factor_ref[...].T), factor_ref[...])
    share = own_ref.shape[0]
    start = lax.axis_index("row") // NC * (NC * share)
    own_ref[...] = whole_ref[pl.ds(pl.multiple_of(start, share), share)]
    other_ref[...] = whole_ref[pl.ds(pl.multiple_of(start + share, share), share)]


def on_device(lhat, ainv_anc, diag_inv, targets):
    slots, height, width = lhat.shape
    core = lax.axis_index("row") % NC
    share = diag_inv.shape[1]
    supers = NX * NZ
    length = (slots + 1) * share
    vmem, hbm = (pl.BlockSpec(memory_space=m) for m in (pltpu.VMEM, pltpu.HBM))

    def here(*lengths, dtype=jnp.float32):
        return pltpu.VMEM(lengths, dtype)

    def on_chip(x):
        return pltpu.with_memory_space_constraint(x, pltpu.VMEM)

    def call(kernel, ins, outs, mib, *args, scratch=()):
        return pl.pallas_call(
            kernel,
            in_specs=ins,
            out_specs=[vmem] * len(outs),
            out_shape=outs,
            scratch_shapes=scratch,
            compiler_params=pltpu.CompilerParams(vmem_limit_bytes=mib << 20),
        )(*args)

    sent, own, held, tile = call(
        sent_kernel,
        [hbm] * 4,
        [
            here(NY, length, width),
            here(2, slots, NY * share, width, dtype=jnp.bfloat16),
            here(slots, height, width),
            here(share, width),
        ],
        24,
        *(
            pltpu.with_memory_space_constraint(x, pltpu.HBM)
            for x in (targets.reshape(slots), lhat, ainv_anc, diag_inv)
        ),
        scratch=[
            pltpu.SMEM((slots,), jnp.int32),
            pltpu.VMEM((1, share, width), jnp.float32),
            pltpu.VMEM((slots, height, width), jnp.float32),
            pltpu.SemaphoreType.DMA((2,)),
            pltpu.SemaphoreType.DMA((2, slots)),
        ],
    )
    arrived = lax.ppermute(sent, BOTH, PARTNER)
    (kept,) = call(kept_kernel, [vmem] * 3, [here(NY, length, width)], 24, on_chip(own), on_chip(held), on_chip(tile))
    own_message, *messages = call(
        place_kernel,
        [vmem] * 2,
        [here(NC, length, width)] * NY,
        24,
        on_chip(kept),
        on_chip(arrived),
    )
    got = [lax.ppermute(message, BOTH, along(shift)) for message, shift in zip(messages, SHIFTS)]

    def numbers(n):
        return [pltpu.SMEM((NC, 1, width), jnp.float32)] * n + [pltpu.SemaphoreType.DMA((n,))]

    results = [here(supers, share, width), here(NY * NC * share, width)]
    partial = call(
        early_kernel,
        [vmem] * (EARLY + 1),
        results,
        24,
        *(on_chip(x) for x in (own_message, *got[:EARLY])),
        scratch=numbers(EARLY + 1),
    )
    summed, factor = call(
        late_kernel,
        [vmem] * (2 + len(SHIFTS) - EARLY),
        results,
        24,
        *(on_chip(x) for x in (*partial, *got[EARLY:])),
        scratch=numbers(len(SHIFTS) - EARLY),
    )

    parts = lax.all_to_all(summed, BOTH, 0, 0, axis_index_groups=PLANES, tiled=True)
    total = jnp.sum(parts, axis=0)
    turned = lax.ppermute(total, BOTH, TURN)

    factor, total = lax.optimization_barrier((factor, total))
    gram, gram_other = call(
        gram_kernel, [vmem], [here(share, width), here(share, width)], 24, on_chip(factor),
        scratch=[pltpu.VMEM((width, width), jnp.float32)],
    )
    gram_odd = lax.ppermute(gram_other, BOTH, TO_ODD)
    return jnp.where(core == 0, gram - total, gram_odd - turned)[None]


def solution(mesh):
    placed = (
        P(("row", "col"), None, None),
        P(("row", "col"), None, None),
        P("col", "row", None),
        P(("row", "col"), None),
    )
    return jax.shard_map(
        on_device, mesh=mesh, in_specs=placed, out_specs=P("col", "row", None), check_vma=False
    )
```

profile of v0, /device:TPU:9, one launch (start us, length us, event | category | flops | bytes accessed | tf_op | source)
XLA Modules:
  0.0 82.5 jit_solution(4169608317808635079)
XLA Ops:
  0.0 3.4 %shard_map.46 = (f32[8,144,256]{2,1,0:T(8,128)S(1)}, bf16[2,8,128,256]{3,2,1,0:T(8,128)(2,1)S(1)}, f32[8,256,256]{2,1,0:T(8,128)S(1)}, f32[16,256]{1,0:T(8,128)S(1)}) custom-call(s32[8]{0:T(128)} %bitcast.3, f32[8,256,256]{2,1,0:T(8,128)} %left_ref.1, f32[8,256,256]{2,1,0:T(8,128)} %right_ref.1, f32[1,16,256]{2,1,0:T(8,128)} %rows_hbm.1), custom_call_target="tpu_custom_call" | custom-call | tf_op jit(solution)/shard_map/pallas_call | solution.py:199
  3.4 2.6 %collective-permute-start = (f32[8,144,256]{2,1,0:T(8,128)S(1)}, f32[8,144,256]{2,1,0:T(8,128)S(1)}, u32[]{:S(2)}, u32[]{:S(2)}) collective-permute-start(f32[8,144,256]{2,1,0:T(8,128)S(1)} %get-tuple-element.28), channel_id=1, source_target_pairs={{0,32},{1,33},{2,34},{3,35},{4,36},{5,37},{6,38},{7,39},{8,40},{9,... | collective-permute-start | bytes 3538952 | tf_op jit(solution)/shard_map/ppermute | solution.py:230
  6.0 0.7 shard_map.47.kept_ref
  6.7 1.8 %collective-permute-done.arrived_ref = f32[8,144,256]{2,1,0:T(8,128)S(1)} collective-permute-done((f32[8,144,256]{2,1,0:T(8,128)S(1)}, f32[8,144,256]{2,1,0:T(8,128)S(1)}, u32[]{:S(2)}, u32[]{:S(2)}) %collective-permute-start) | collective-permute-done | bytes 1179680 | tf_op jit(solution)/shard_map/ppermute | solution.py:230
  8.5 0.2 shard_map.48
  8.6 10.6 %collective-permute-start.1 = (f32[2,144,256]{2,1,0:T(8,128)S(1)}, f32[2,144,256]{2,1,0:T(8,128)S(1)}, u32[]{:S(2)}, u32[]{:S(2)}) collective-permute-start(f32[2,144,256]{2,1,0:T(8,128)S(1)} %get-tuple-element.30), channel_id=1, source_target_pairs={{0,256},{1,257},{2,258},{3,259},{4,260},{5,261},{6,262},{7,263},{8... | collective-permute-start | bytes 884744 | tf_op jit(solution)/shard_map/ppermute | solution.py:240
  19.3 4.9 %collective-permute-start.2 = (f32[2,144,256]{2,1,0:T(8,128)S(1)}, f32[2,144,256]{2,1,0:T(8,128)S(1)}, u32[]{:S(2)}, u32[]{:S(2)}) collective-permute-start(f32[2,144,256]{2,1,0:T(8,128)S(1)} %get-tuple-element.31), channel_id=1, source_target_pairs={{0,192},{1,193},{2,194},{3,195},{4,196},{5,197},{6,198},{7,199},{8... | collective-permute-start | bytes 884744 | tf_op jit(solution)/shard_map/ppermute | solution.py:240
  24.2 3.4 %collective-permute-start.3 = (f32[2,144,256]{2,1,0:T(8,128)S(1)}, f32[2,144,256]{2,1,0:T(8,128)S(1)}, u32[]{:S(2)}, u32[]{:S(2)}) collective-permute-start(f32[2,144,256]{2,1,0:T(8,128)S(1)} %get-tuple-element.32), channel_id=1, source_target_pairs={{0,320},{1,321},{2,322},{3,323},{4,324},{5,325},{6,326},{7,327},{8... | collective-permute-start | bytes 884744 | tf_op jit(solution)/shard_map/ppermute | solution.py:240
  27.6 4.0 %collective-permute-start.4 = (f32[2,144,256]{2,1,0:T(8,128)S(1)}, f32[2,144,256]{2,1,0:T(8,128)S(1)}, u32[]{:S(2)}, u32[]{:S(2)}) collective-permute-start(f32[2,144,256]{2,1,0:T(8,128)S(1)} %get-tuple-element.33), channel_id=1, source_target_pairs={{0,128},{1,129},{2,130},{3,131},{4,132},{5,133},{6,134},{7,135},{8... | collective-permute-start | bytes 884744 | tf_op jit(solution)/shard_map/ppermute | solution.py:240
  31.6 3.4 %collective-permute-start.5 = (f32[2,144,256]{2,1,0:T(8,128)S(1)}, f32[2,144,256]{2,1,0:T(8,128)S(1)}, u32[]{:S(2)}, u32[]{:S(2)}) collective-permute-start(f32[2,144,256]{2,1,0:T(8,128)S(1)} %get-tuple-element.36), channel_id=1, source_target_pairs={{0,384},{1,385},{2,386},{3,387},{4,388},{5,389},{6,390},{7,391},{8... | collective-permute-start | bytes 884744 | tf_op jit(solution)/shard_map/ppermute | solution.py:240
  35.0 0.0 collective-permute-done.1.refs_1_
  35.0 3.1 %collective-permute-start.6 = (f32[2,144,256]{2,1,0:T(8,128)S(1)}, f32[2,144,256]{2,1,0:T(8,128)S(1)}, u32[]{:S(2)}, u32[]{:S(2)}) collective-permute-start(f32[2,144,256]{2,1,0:T(8,128)S(1)} %get-tuple-element.37), channel_id=1, source_target_pairs={{0,64},{1,65},{2,66},{3,67},{4,68},{5,69},{6,70},{7,71},{8,72},{9,... | collective-permute-start | bytes 884744 | tf_op jit(solution)/shard_map/ppermute | solution.py:240
  38.1 2.8 %collective-permute-done.2.refs_2_ = f32[2,144,256]{2,1,0:T(8,128)S(1)} collective-permute-done((f32[2,144,256]{2,1,0:T(8,128)S(1)}, f32[2,144,256]{2,1,0:T(8,128)S(1)}, u32[]{:S(2)}, u32[]{:S(2)}) %collective-permute-start.2) | collective-permute-done | bytes 294944 | tf_op jit(solution)/shard_map/ppermute | solution.py:240
  40.9 1.9 %collective-permute-start.7 = (f32[2,144,256]{2,1,0:T(8,128)S(1)}, f32[2,144,256]{2,1,0:T(8,128)S(1)}, u32[]{:S(2)}, u32[]{:S(2)}) collective-permute-start(f32[2,144,256]{2,1,0:T(8,128)S(1)} %get-tuple-element.38), channel_id=1, source_target_pairs={{0,448},{1,449},{2,450},{3,451},{4,452},{5,453},{6,454},{7,455},{8... | collective-permute-start | bytes 884744 | tf_op jit(solution)/shard_map/ppermute | solution.py:240
  42.8 0.0 collective-permute-done.3.refs_3_
  42.8 0.0 collective-permute-done.4.refs_4_
  42.8 1.2 %shard_map.49 = (f32[32,16,256]{2,1,0:T(8,128)S(1)}, f32[256,256]{1,0:T(8,128)S(1)}) custom-call(f32[2,144,256]{2,1,0:T(8,128)S(1)} %get-tuple-element.29.refs_0_, f32[2,144,256]{2,1,0:T(8,128)S(1)} %collective-permute-done.1.refs_1_, f32[2,144,256]{2,1,0:T(8,128)S(1)} %collective-permute-done.2.refs_2_, f32[2,144,256]{2,1,0:T(8,128)S(1)} %collective-permute-done.3.refs_3_, ...), custom_call_target="tpu_custom_call" | custom-call | tf_op jit(solution)/shard_map/pallas_call | solution.py:199
  44.1 1.5 %collective-permute-done.5.refs_0_ = f32[2,144,256]{2,1,0:T(8,128)S(1)} collective-permute-done((f32[2,144,256]{2,1,0:T(8,128)S(1)}, f32[2,144,256]{2,1,0:T(8,128)S(1)}, u32[]{:S(2)}, u32[]{:S(2)}) %collective-permute-start.5) | collective-permute-done | bytes 294944 | tf_op jit(solution)/shard_map/ppermute | solution.py:240
  45.5 1.4 %collective-permute-done.6.refs_1_ = f32[2,144,256]{2,1,0:T(8,128)S(1)} collective-permute-done((f32[2,144,256]{2,1,0:T(8,128)S(1)}, f32[2,144,256]{2,1,0:T(8,128)S(1)}, u32[]{:S(2)}, u32[]{:S(2)}) %collective-permute-start.6) | collective-permute-done | bytes 294944 | tf_op jit(solution)/shard_map/ppermute | solution.py:240
  46.9 1.8 %collective-permute-done.7.refs_2_ = f32[2,144,256]{2,1,0:T(8,128)S(1)} collective-permute-done((f32[2,144,256]{2,1,0:T(8,128)S(1)}, f32[2,144,256]{2,1,0:T(8,128)S(1)}, u32[]{:S(2)}, u32[]{:S(2)}) %collective-permute-start.7) | collective-permute-done | bytes 294944 | tf_op jit(solution)/shard_map/ppermute | solution.py:240
  48.7 1.0 %shard_map.50 = (f32[32,16,256]{2,1,0:T(8,128)S(1)}, f32[256,256]{1,0:T(8,128)S(1)}) custom-call(f32[32,16,256]{2,1,0:T(8,128)S(1)} %get-tuple-element.34.sum_ref, f32[256,256]{1,0:T(8,128)S(1)} %get-tuple-element.35.rows_ref, f32[2,144,256]{2,1,0:T(8,128)S(1)} %collective-permute-done.5.refs_0_, f32[2,144,256]{2,1,0:T(8,128)S(1)} %collective-permute-done.6.refs_1_, ...), custom_call_target="tpu_custom_call" | custom-call | tf_op jit(solution)/shard_map/pallas_call | solution.py:199
  49.7 22.0 %all_to_all.5 = f32[32,16,256]{2,1,0:T(8,128)S(1)} all-to-all(f32[32,16,256]{2,1,0:T(8,128)S(1)} %get-tuple-element.40), channel_id=1, replica_groups={{0,1,2,3,4,5,6,7,8,9,10,11,12,13,14,15,16,17,18,19,20,21,22,23,24,25,26..., dimensions={0} | all-to-all | bytes 1048576 | tf_op jit(solution)/shard_map/all_to_all | solution.py:263
  71.7 0.3 shard_map.51
  72.0 1.3 %collective-permute-start.8 = (f32[16,256]{1,0:T(8,128)S(1)}, f32[16,256]{1,0:T(8,128)S(1)}, u32[]{:S(2)}, u32[]{:S(2)}) collective-permute-start(f32[16,256]{1,0:T(8,128)S(1)} %get-tuple-element.44), channel_id=1, source_target_pairs={{0,32},{1,33},{2,34},{3,35},{4,36},{5,37},{6,38},{7,39},{8,40},{9,... | collective-permute-start | bytes 49160 | tf_op jit(solution)/shard_map/ppermute | solution.py:272
  73.3 3.9 %collective-permute-start.9 = (f32[16,256]{1,0:T(8,128)S(1)}, f32[16,256]{1,0:T(8,128)S(1)}, u32[]{:S(2)}, u32[]{:S(2)}) collective-permute-start(f32[16,256]{1,0:T(8,128)S(1)} %reduce_sum.9), channel_id=1, source_target_pairs={{32,36},{33,100},{34,164},{35,228},{36,292},{37,356},{38,420},{39,... | collective-permute-start | bytes 49160 | tf_op jit(solution)/shard_map/ppermute | solution.py:265
  77.3 0.0 collective-permute-done.8
  77.3 4.6 %collective-permute-done.9 = f32[16,256]{1,0:T(8,128)S(1)} collective-permute-done((f32[16,256]{1,0:T(8,128)S(1)}, f32[16,256]{1,0:T(8,128)S(1)}, u32[]{:S(2)}, u32[]{:S(2)}) %collective-permute-start.9) | collective-permute-done | bytes 16416 | tf_op jit(solution)/shard_map/ppermute | solution.py:265
  81.9 0.6 select_bitcast_fusion
  (1 shorter events, 0.0 us)
Async XLA Ops:
  3.4 5.0 %collective-permute-start = (f32[8,144,256]{2,1,0:T(8,128)S(1)}, f32[8,144,256]{2,1,0:T(8,128)S(1)}, u32[]{:S(2)}, u32[]{:S(2)}) collective-permute-start(f32[8,144,256]{2,1,0:T(8,128)S(1)} %get-tuple-element.28), channel_id=1, source_target_pairs={{0,32},{1,33},{2,34},{3,35},{4,36},{5,37},{6,38},{7,39},{8,40},{9,... | collective-permute-start | bytes 3538952 | tf_op jit(solution)/shard_map/ppermute | solution.py:230
  8.6 26.4 %collective-permute-start.1 = (f32[2,144,256]{2,1,0:T(8,128)S(1)}, f32[2,144,256]{2,1,0:T(8,128)S(1)}, u32[]{:S(2)}, u32[]{:S(2)}) collective-permute-start(f32[2,144,256]{2,1,0:T(8,128)S(1)} %get-tuple-element.30), channel_id=1, source_target_pairs={{0,256},{1,257},{2,258},{3,259},{4,260},{5,261},{6,262},{7,263},{8... | collective-permute-start | bytes 884744 | tf_op jit(solution)/shard_map/ppermute | solution.py:240
  19.3 21.6 %collective-permute-start.2 = (f32[2,144,256]{2,1,0:T(8,128)S(1)}, f32[2,144,256]{2,1,0:T(8,128)S(1)}, u32[]{:S(2)}, u32[]{:S(2)}) collective-permute-start(f32[2,144,256]{2,1,0:T(8,128)S(1)} %get-tuple-element.31), channel_id=1, source_target_pairs={{0,192},{1,193},{2,194},{3,195},{4,196},{5,197},{6,198},{7,199},{8... | collective-permute-start | bytes 884744 | tf_op jit(solution)/shard_map/ppermute | solution.py:240
  24.2 18.6 %collective-permute-start.3 = (f32[2,144,256]{2,1,0:T(8,128)S(1)}, f32[2,144,256]{2,1,0:T(8,128)S(1)}, u32[]{:S(2)}, u32[]{:S(2)}) collective-permute-start(f32[2,144,256]{2,1,0:T(8,128)S(1)} %get-tuple-element.32), channel_id=1, source_target_pairs={{0,320},{1,321},{2,322},{3,323},{4,324},{5,325},{6,326},{7,327},{8... | collective-permute-start | bytes 884744 | tf_op jit(solution)/shard_map/ppermute | solution.py:240
  27.6 15.2 %collective-permute-start.4 = (f32[2,144,256]{2,1,0:T(8,128)S(1)}, f32[2,144,256]{2,1,0:T(8,128)S(1)}, u32[]{:S(2)}, u32[]{:S(2)}) collective-permute-start(f32[2,144,256]{2,1,0:T(8,128)S(1)} %get-tuple-element.33), channel_id=1, source_target_pairs={{0,128},{1,129},{2,130},{3,131},{4,132},{5,133},{6,134},{7,135},{8... | collective-permute-start | bytes 884744 | tf_op jit(solution)/shard_map/ppermute | solution.py:240
  31.6 13.9 %collective-permute-start.5 = (f32[2,144,256]{2,1,0:T(8,128)S(1)}, f32[2,144,256]{2,1,0:T(8,128)S(1)}, u32[]{:S(2)}, u32[]{:S(2)}) collective-permute-start(f32[2,144,256]{2,1,0:T(8,128)S(1)} %get-tuple-element.36), channel_id=1, source_target_pairs={{0,384},{1,385},{2,386},{3,387},{4,388},{5,389},{6,390},{7,391},{8... | collective-permute-start | bytes 884744 | tf_op jit(solution)/shard_map/ppermute | solution.py:240
  35.0 11.9 %collective-permute-start.6 = (f32[2,144,256]{2,1,0:T(8,128)S(1)}, f32[2,144,256]{2,1,0:T(8,128)S(1)}, u32[]{:S(2)}, u32[]{:S(2)}) collective-permute-start(f32[2,144,256]{2,1,0:T(8,128)S(1)} %get-tuple-element.37), channel_id=1, source_target_pairs={{0,64},{1,65},{2,66},{3,67},{4,68},{5,69},{6,70},{7,71},{8,72},{9,... | collective-permute-start | bytes 884744 | tf_op jit(solution)/shard_map/ppermute | solution.py:240
  40.9 7.8 %collective-permute-start.7 = (f32[2,144,256]{2,1,0:T(8,128)S(1)}, f32[2,144,256]{2,1,0:T(8,128)S(1)}, u32[]{:S(2)}, u32[]{:S(2)}) collective-permute-start(f32[2,144,256]{2,1,0:T(8,128)S(1)} %get-tuple-element.38), channel_id=1, source_target_pairs={{0,448},{1,449},{2,450},{3,451},{4,452},{5,453},{6,454},{7,455},{8... | collective-permute-start | bytes 884744 | tf_op jit(solution)/shard_map/ppermute | solution.py:240
  72.0 5.2 %collective-permute-start.8 = (f32[16,256]{1,0:T(8,128)S(1)}, f32[16,256]{1,0:T(8,128)S(1)}, u32[]{:S(2)}, u32[]{:S(2)}) collective-permute-start(f32[16,256]{1,0:T(8,128)S(1)} %get-tuple-element.44), channel_id=1, source_target_pairs={{0,32},{1,33},{2,34},{3,35},{4,36},{5,37},{6,38},{7,39},{8,40},{9,... | collective-permute-start | bytes 49160 | tf_op jit(solution)/shard_map/ppermute | solution.py:272
  73.3 8.6 %collective-permute-start.9 = (f32[16,256]{1,0:T(8,128)S(1)}, f32[16,256]{1,0:T(8,128)S(1)}, u32[]{:S(2)}, u32[]{:S(2)}) collective-permute-start(f32[16,256]{1,0:T(8,128)S(1)} %reduce_sum.9), channel_id=1, source_target_pairs={{32,36},{33,100},{34,164},{35,228},{36,292},{37,356},{38,420},{39,... | collective-permute-start | bytes 49160 | tf_op jit(solution)/shard_map/ppermute | solution.py:265
where the time goes:
time: 82.9 us; the launch traced here: 82.5 us
  starting transfers between devices  39.1 us (47%)
  blocking collectives  22 us (27%)
  waiting for transfers between devices  13.9 us (17%)
  Pallas kernels  6.73 us (8%)
    ppermute x7, starting transfers between devices, on_device(): lax.ppermute(message, BOTH, along(shift))  31.3 us
    all_to_all x1, blocking collectives, on_device(): lax.all_to_all(summed, BOTH, 0, 0, axis_index_groups=PLANES, tiled=True)  22 us
    ppermute x7, waiting for transfers between devices, on_device(): lax.ppermute(message, BOTH, along(shift))  7.46 us
    pallas_call x6, Pallas kernels, call(): pl.pallas_call(kernel, in_specs=ins, out_specs=[vmem] * len(outs), out_sh...  6.73 us
    ppermute x1, waiting for transfers between devices, on_device(): turned = lax.ppermute(total, BOTH, TURN)  4.64 us
    ppermute x1, starting transfers between devices, on_device(): turned = lax.ppermute(total, BOTH, TURN)  3.9 us
    ppermute x1, starting transfers between devices, on_device(): arrived = lax.ppermute(sent, BOTH, PARTNER)  2.58 us
    ppermute x1, waiting for transfers between devices, on_device(): arrived = lax.ppermute(sent, BOTH, PARTNER)  1.79 us
  transfers between devices with their start and end apart: 10, of which 6 were waited for; matrix products, arithmetic and copies ran while one was open for 0% of the time, Pallas kernels for 2%

commit v1 on v0

--- a/solution.py
+++ b/solution.py
@@ -22,7 +22,7 @@
     [flat(y, 1, x, z) for x in range(NX) for y in range(NY)] for z in range(NZ)
 ]
 SHIFTS = (4, 3, 5, 2, 6, 1, 7)
-EARLY = 4
+EARLY = 5
 
 
 def along(shift):
@@ -121,7 +121,7 @@
         out_ref[1] = arrived_ref[(me + shift) % NY]
 
 
-def add_blocks(shifts, got_refs, ids_refs, sems, out_ref, factor_ref):
+def add_blocks(shifts, got_refs, ids_refs, sems, out_ref, factor_ref, summed, rows):
     share = out_ref.shape[1]
     slots = got_refs[0].shape[1] // share - 1
     base = slots * share
@@ -131,6 +131,8 @@
     ]
     for copy in copies:
         copy.start()
+    out_ref[...] = summed()
+    factor_ref[...] = rows()
     index = lax.axis_index("row")
     core = index % NC
     flip = core * FAR
@@ -160,17 +162,15 @@
 def early_kernel(*refs):
     n = EARLY + 1
     got_refs, (out_ref, factor_ref), ids_refs, sems = refs[:n], refs[n : n + 2], refs[n + 2 : -1], refs[-1]
-    out_ref[...] = jnp.zeros_like(out_ref)
-    factor_ref[...] = jnp.zeros_like(factor_ref)
-    add_blocks((0, *SHIFTS[:EARLY]), got_refs, ids_refs, sems, out_ref, factor_ref)
+    zeros = (lambda: jnp.zeros_like(out_ref), lambda: jnp.zeros_like(factor_ref))
+    add_blocks((0, *SHIFTS[:EARLY]), got_refs, ids_refs, sems, out_ref, factor_ref, *zeros)
 
 
 def late_kernel(sum_ref, rows_ref, *refs):
     n = len(SHIFTS) - EARLY
     got_refs, (out_ref, factor_ref), ids_refs, sems = refs[:n], refs[n : n + 2], refs[n + 2 : -1], refs[-1]
-    out_ref[...] = sum_ref[...]
-    factor_ref[...] = rows_ref[...]
-    add_blocks(SHIFTS[EARLY:], got_refs, ids_refs, sems, out_ref, factor_ref)
+    before = (lambda: sum_ref[...], lambda: rows_ref[...])
+    add_blocks(SHIFTS[EARLY:], got_refs, ids_refs, sems, out_ref, factor_ref, *before)
 
 
 def gram_kernel(factor_ref, own_ref, other_ref, whole_ref):

time: 82.9 us -> 82.7 us (level)
  no operation moved by 1% of the time
where the time goes in v1:
time: 82.7 us; the launch traced here: 82.3 us
  starting transfers between devices  39.1 us (47%)
  blocking collectives  22 us (27%)
  waiting for transfers between devices  13.8 us (17%)
  Pallas kernels  6.63 us (8%)
    ppermute x7, starting transfers between devices, on_device(): lax.ppermute(message, BOTH, along(shift))  31.3 us
    all_to_all x1, blocking collectives, on_device(): lax.all_to_all(summed, BOTH, 0, 0, axis_index_groups=PLANES, tiled=True)  22 us
    ppermute x7, waiting for transfers between devices, on_device(): lax.ppermute(message, BOTH, along(shift))  7.38 us
    pallas_call x6, Pallas kernels, call(): pl.pallas_call(kernel, in_specs=ins, out_specs=[vmem] * len(outs), out_sh...  6.63 us
    ppermute x1, waiting for transfers between devices, on_device(): turned = lax.ppermute(total, BOTH, TURN)  4.64 us
    ppermute x1, starting transfers between devices, on_device(): turned = lax.ppermute(total, BOTH, TURN)  3.9 us
    ppermute x1, starting transfers between devices, on_device(): arrived = lax.ppermute(sent, BOTH, PARTNER)  2.58 us
    ppermute x1, waiting for transfers between devices, on_device(): arrived = lax.ppermute(sent, BOTH, PARTNER)  1.79 us
  transfers between devices with their start and end apart: 10, of which 6 were waited for; matrix products, arithmetic and copies ran while one was open for 0% of the time, Pallas kernels for 2%

profile of v1, /device:TPU:9, one launch (start us, length us, event | category | flops | bytes accessed | tf_op | source)
XLA Modules:
  0.0 82.3 jit_solution(14563192278742924822)
XLA Ops:
  0.0 3.4 %shard_map.46 = (f32[8,144,256]{2,1,0:T(8,128)S(1)}, bf16[2,8,128,256]{3,2,1,0:T(8,128)(2,1)S(1)}, f32[8,256,256]{2,1,0:T(8,128)S(1)}, f32[16,256]{1,0:T(8,128)S(1)}) custom-call(s32[8]{0:T(128)} %bitcast.3, f32[8,256,256]{2,1,0:T(8,128)} %left_ref.1, f32[8,256,256]{2,1,0:T(8,128)} %right_ref.1, f32[1,16,256]{2,1,0:T(8,128)} %rows_hbm.1), custom_call_target="tpu_custom_call" | custom-call | tf_op jit(solution)/shard_map/pallas_call | solution.py:199
  3.4 2.6 %collective-permute-start = (f32[8,144,256]{2,1,0:T(8,128)S(1)}, f32[8,144,256]{2,1,0:T(8,128)S(1)}, u32[]{:S(2)}, u32[]{:S(2)}) collective-permute-start(f32[8,144,256]{2,1,0:T(8,128)S(1)} %get-tuple-element.28), channel_id=1, source_target_pairs={{0,32},{1,33},{2,34},{3,35},{4,36},{5,37},{6,38},{7,39},{8,40},{9,... | collective-permute-start | bytes 3538952 | tf_op jit(solution)/shard_map/ppermute | solution.py:230
  6.0 0.7 shard_map.47.kept_ref
  6.7 1.8 %collective-permute-done.arrived_ref = f32[8,144,256]{2,1,0:T(8,128)S(1)} collective-permute-done((f32[8,144,256]{2,1,0:T(8,128)S(1)}, f32[8,144,256]{2,1,0:T(8,128)S(1)}, u32[]{:S(2)}, u32[]{:S(2)}) %collective-permute-start) | collective-permute-done | bytes 1179680 | tf_op jit(solution)/shard_map/ppermute | solution.py:230
  8.5 0.2 shard_map.48
  8.6 10.6 %collective-permute-start.1 = (f32[2,144,256]{2,1,0:T(8,128)S(1)}, f32[2,144,256]{2,1,0:T(8,128)S(1)}, u32[]{:S(2)}, u32[]{:S(2)}) collective-permute-start(f32[2,144,256]{2,1,0:T(8,128)S(1)} %get-tuple-element.30), channel_id=1, source_target_pairs={{0,256},{1,257},{2,258},{3,259},{4,260},{5,261},{6,262},{7,263},{8... | collective-permute-start | bytes 884744 | tf_op jit(solution)/shard_map/ppermute | solution.py:240
  19.3 4.9 %collective-permute-start.2 = (f32[2,144,256]{2,1,0:T(8,128)S(1)}, f32[2,144,256]{2,1,0:T(8,128)S(1)}, u32[]{:S(2)}, u32[]{:S(2)}) collective-permute-start(f32[2,144,256]{2,1,0:T(8,128)S(1)} %get-tuple-element.31), channel_id=1, source_target_pairs={{0,192},{1,193},{2,194},{3,195},{4,196},{5,197},{6,198},{7,199},{8... | collective-permute-start | bytes 884744 | tf_op jit(solution)/shard_map/ppermute | solution.py:240
  24.2 3.4 %collective-permute-start.3 = (f32[2,144,256]{2,1,0:T(8,128)S(1)}, f32[2,144,256]{2,1,0:T(8,128)S(1)}, u32[]{:S(2)}, u32[]{:S(2)}) collective-permute-start(f32[2,144,256]{2,1,0:T(8,128)S(1)} %get-tuple-element.32), channel_id=1, source_target_pairs={{0,320},{1,321},{2,322},{3,323},{4,324},{5,325},{6,326},{7,327},{8... | collective-permute-start | bytes 884744 | tf_op jit(solution)/shard_map/ppermute | solution.py:240
  27.6 4.0 %collective-permute-start.4 = (f32[2,144,256]{2,1,0:T(8,128)S(1)}, f32[2,144,256]{2,1,0:T(8,128)S(1)}, u32[]{:S(2)}, u32[]{:S(2)}) collective-permute-start(f32[2,144,256]{2,1,0:T(8,128)S(1)} %get-tuple-element.33), channel_id=1, source_target_pairs={{0,128},{1,129},{2,130},{3,131},{4,132},{5,133},{6,134},{7,135},{8... | collective-permute-start | bytes 884744 | tf_op jit(solution)/shard_map/ppermute | solution.py:240
  31.6 3.4 %collective-permute-start.5 = (f32[2,144,256]{2,1,0:T(8,128)S(1)}, f32[2,144,256]{2,1,0:T(8,128)S(1)}, u32[]{:S(2)}, u32[]{:S(2)}) collective-permute-start(f32[2,144,256]{2,1,0:T(8,128)S(1)} %get-tuple-element.34), channel_id=1, source_target_pairs={{0,384},{1,385},{2,386},{3,387},{4,388},{5,389},{6,390},{7,391},{8... | collective-permute-start | bytes 884744 | tf_op jit(solution)/shard_map/ppermute | solution.py:240
  35.0 0.0 collective-permute-done.1.refs_1_
  35.0 3.1 %collective-permute-start.6 = (f32[2,144,256]{2,1,0:T(8,128)S(1)}, f32[2,144,256]{2,1,0:T(8,128)S(1)}, u32[]{:S(2)}, u32[]{:S(2)}) collective-permute-start(f32[2,144,256]{2,1,0:T(8,128)S(1)} %get-tuple-element.37), channel_id=1, source_target_pairs={{0,64},{1,65},{2,66},{3,67},{4,68},{5,69},{6,70},{7,71},{8,72},{9,... | collective-permute-start | bytes 884744 | tf_op jit(solution)/shard_map/ppermute | solution.py:240
  38.1 2.8 %collective-permute-done.2.refs_2_ = f32[2,144,256]{2,1,0:T(8,128)S(1)} collective-permute-done((f32[2,144,256]{2,1,0:T(8,128)S(1)}, f32[2,144,256]{2,1,0:T(8,128)S(1)}, u32[]{:S(2)}, u32[]{:S(2)}) %collective-permute-start.2) | collective-permute-done | bytes 294944 | tf_op jit(solution)/shard_map/ppermute | solution.py:240
  40.9 1.9 %collective-permute-start.7 = (f32[2,144,256]{2,1,0:T(8,128)S(1)}, f32[2,144,256]{2,1,0:T(8,128)S(1)}, u32[]{:S(2)}, u32[]{:S(2)}) collective-permute-start(f32[2,144,256]{2,1,0:T(8,128)S(1)} %get-tuple-element.38), channel_id=1, source_target_pairs={{0,448},{1,449},{2,450},{3,451},{4,452},{5,453},{6,454},{7,455},{8... | collective-permute-start | bytes 884744 | tf_op jit(solution)/shard_map/ppermute | solution.py:240
  42.8 0.0 collective-permute-done.3.refs_3_
  42.8 0.0 collective-permute-done.4.refs_4_
  42.8 2.7 %collective-permute-done.5.refs_5_ = f32[2,144,256]{2,1,0:T(8,128)S(1)} collective-permute-done((f32[2,144,256]{2,1,0:T(8,128)S(1)}, f32[2,144,256]{2,1,0:T(8,128)S(1)}, u32[]{:S(2)}, u32[]{:S(2)}) %collective-permute-start.5) | collective-permute-done | bytes 294944 | tf_op jit(solution)/shard_map/ppermute | solution.py:240
  45.5 1.3 %shard_map.49 = (f32[32,16,256]{2,1,0:T(8,128)S(1)}, f32[256,256]{1,0:T(8,128)S(1)}) custom-call(f32[2,144,256]{2,1,0:T(8,128)S(1)} %get-tuple-element.29.refs_0_, f32[2,144,256]{2,1,0:T(8,128)S(1)} %collective-permute-done.1.refs_1_, f32[2,144,256]{2,1,0:T(8,128)S(1)} %collective-permute-done.2.refs_2_, f32[2,144,256]{2,1,0:T(8,128)S(1)} %collective-permute-done.3.refs_3_, ...), custom_call_target="tpu_custom_call" | custom-call | tf_op jit(solution)/shard_map/pallas_call | solution.py:199
  46.8 0.1 collective-permute-done.6.refs_0_
  46.9 1.8 %collective-permute-done.7.refs_1_ = f32[2,144,256]{2,1,0:T(8,128)S(1)} collective-permute-done((f32[2,144,256]{2,1,0:T(8,128)S(1)}, f32[2,144,256]{2,1,0:T(8,128)S(1)}, u32[]{:S(2)}, u32[]{:S(2)}) %collective-permute-start.7) | collective-permute-done | bytes 294944 | tf_op jit(solution)/shard_map/ppermute | solution.py:240
  48.7 0.8 shard_map.50
  49.5 22.0 %all_to_all.5 = f32[32,16,256]{2,1,0:T(8,128)S(1)} all-to-all(f32[32,16,256]{2,1,0:T(8,128)S(1)} %get-tuple-element.40), channel_id=1, replica_groups={{0,1,2,3,4,5,6,7,8,9,10,11,12,13,14,15,16,17,18,19,20,21,22,23,24,25,26..., dimensions={0} | all-to-all | bytes 1048576 | tf_op jit(solution)/shard_map/all_to_all | solution.py:263
  71.5 0.3 shard_map.51
  71.9 1.3 %collective-permute-start.8 = (f32[16,256]{1,0:T(8,128)S(1)}, f32[16,256]{1,0:T(8,128)S(1)}, u32[]{:S(2)}, u32[]{:S(2)}) collective-permute-start(f32[16,256]{1,0:T(8,128)S(1)} %get-tuple-element.44), channel_id=1, source_target_pairs={{0,32},{1,33},{2,34},{3,35},{4,36},{5,37},{6,38},{7,39},{8,40},{9,... | collective-permute-start | bytes 49160 | tf_op jit(solution)/shard_map/ppermute | solution.py:272
  73.2 3.9 %collective-permute-start.9 = (f32[16,256]{1,0:T(8,128)S(1)}, f32[16,256]{1,0:T(8,128)S(1)}, u32[]{:S(2)}, u32[]{:S(2)}) collective-permute-start(f32[16,256]{1,0:T(8,128)S(1)} %reduce_sum.9), channel_id=1, source_target_pairs={{32,36},{33,100},{34,164},{35,228},{36,292},{37,356},{38,420},{39,... | collective-permute-start | bytes 49160 | tf_op jit(solution)/shard_map/ppermute | solution.py:265
  77.1 0.0 collective-permute-done.8
  77.1 4.6 %collective-permute-done.9 = f32[16,256]{1,0:T(8,128)S(1)} collective-permute-done((f32[16,256]{1,0:T(8,128)S(1)}, f32[16,256]{1,0:T(8,128)S(1)}, u32[]{:S(2)}, u32[]{:S(2)}) %collective-permute-start.9) | collective-permute-done | bytes 16416 | tf_op jit(solution)/shard_map/ppermute | solution.py:265
  81.7 0.6 select_bitcast_fusion
  (1 shorter events, 0.0 us)
Async XLA Ops:
  3.4 5.0 %collective-permute-start = (f32[8,144,256]{2,1,0:T(8,128)S(1)}, f32[8,144,256]{2,1,0:T(8,128)S(1)}, u32[]{:S(2)}, u32[]{:S(2)}) collective-permute-start(f32[8,144,256]{2,1,0:T(8,128)S(1)} %get-tuple-element.28), channel_id=1, source_target_pairs={{0,32},{1,33},{2,34},{3,35},{4,36},{5,37},{6,38},{7,39},{8,40},{9,... | collective-permute-start | bytes 3538952 | tf_op jit(solution)/shard_map/ppermute | solution.py:230
  8.6 26.4 %collective-permute-start.1 = (f32[2,144,256]{2,1,0:T(8,128)S(1)}, f32[2,144,256]{2,1,0:T(8,128)S(1)}, u32[]{:S(2)}, u32[]{:S(2)}) collective-permute-start(f32[2,144,256]{2,1,0:T(8,128)S(1)} %get-tuple-element.30), channel_id=1, source_target_pairs={{0,256},{1,257},{2,258},{3,259},{4,260},{5,261},{6,262},{7,263},{8... | collective-permute-start | bytes 884744 | tf_op jit(solution)/shard_map/ppermute | solution.py:240
  19.3 21.6 %collective-permute-start.2 = (f32[2,144,256]{2,1,0:T(8,128)S(1)}, f32[2,144,256]{2,1,0:T(8,128)S(1)}, u32[]{:S(2)}, u32[]{:S(2)}) collective-permute-start(f32[2,144,256]{2,1,0:T(8,128)S(1)} %get-tuple-element.31), channel_id=1, source_target_pairs={{0,192},{1,193},{2,194},{3,195},{4,196},{5,197},{6,198},{7,199},{8... | collective-permute-start | bytes 884744 | tf_op jit(solution)/shard_map/ppermute | solution.py:240
  24.2 18.6 %collective-permute-start.3 = (f32[2,144,256]{2,1,0:T(8,128)S(1)}, f32[2,144,256]{2,1,0:T(8,128)S(1)}, u32[]{:S(2)}, u32[]{:S(2)}) collective-permute-start(f32[2,144,256]{2,1,0:T(8,128)S(1)} %get-tuple-element.32), channel_id=1, source_target_pairs={{0,320},{1,321},{2,322},{3,323},{4,324},{5,325},{6,326},{7,327},{8... | collective-permute-start | bytes 884744 | tf_op jit(solution)/shard_map/ppermute | solution.py:240
  27.6 15.2 %collective-permute-start.4 = (f32[2,144,256]{2,1,0:T(8,128)S(1)}, f32[2,144,256]{2,1,0:T(8,128)S(1)}, u32[]{:S(2)}, u32[]{:S(2)}) collective-permute-start(f32[2,144,256]{2,1,0:T(8,128)S(1)} %get-tuple-element.33), channel_id=1, source_target_pairs={{0,128},{1,129},{2,130},{3,131},{4,132},{5,133},{6,134},{7,135},{8... | collective-permute-start | bytes 884744 | tf_op jit(solution)/shard_map/ppermute | solution.py:240
  31.6 13.9 %collective-permute-start.5 = (f32[2,144,256]{2,1,0:T(8,128)S(1)}, f32[2,144,256]{2,1,0:T(8,128)S(1)}, u32[]{:S(2)}, u32[]{:S(2)}) collective-permute-start(f32[2,144,256]{2,1,0:T(8,128)S(1)} %get-tuple-element.34), channel_id=1, source_target_pairs={{0,384},{1,385},{2,386},{3,387},{4,388},{5,389},{6,390},{7,391},{8... | collective-permute-start | bytes 884744 | tf_op jit(solution)/shard_map/ppermute | solution.py:240
  35.0 11.9 %collective-permute-start.6 = (f32[2,144,256]{2,1,0:T(8,128)S(1)}, f32[2,144,256]{2,1,0:T(8,128)S(1)}, u32[]{:S(2)}, u32[]{:S(2)}) collective-permute-start(f32[2,144,256]{2,1,0:T(8,128)S(1)} %get-tuple-element.37), channel_id=1, source_target_pairs={{0,64},{1,65},{2,66},{3,67},{4,68},{5,69},{6,70},{7,71},{8,72},{9,... | collective-permute-start | bytes 884744 | tf_op jit(solution)/shard_map/ppermute | solution.py:240
  40.9 7.8 %collective-permute-start.7 = (f32[2,144,256]{2,1,0:T(8,128)S(1)}, f32[2,144,256]{2,1,0:T(8,128)S(1)}, u32[]{:S(2)}, u32[]{:S(2)}) collective-permute-start(f32[2,144,256]{2,1,0:T(8,128)S(1)} %get-tuple-element.38), channel_id=1, source_target_pairs={{0,448},{1,449},{2,450},{3,451},{4,452},{5,453},{6,454},{7,455},{8... | collective-permute-start | bytes 884744 | tf_op jit(solution)/shard_map/ppermute | solution.py:240
  71.9 5.2 %collective-permute-start.8 = (f32[16,256]{1,0:T(8,128)S(1)}, f32[16,256]{1,0:T(8,128)S(1)}, u32[]{:S(2)}, u32[]{:S(2)}) collective-permute-start(f32[16,256]{1,0:T(8,128)S(1)} %get-tuple-element.44), channel_id=1, source_target_pairs={{0,32},{1,33},{2,34},{3,35},{4,36},{5,37},{6,38},{7,39},{8,40},{9,... | collective-permute-start | bytes 49160 | tf_op jit(solution)/shard_map/ppermute | solution.py:272
  73.2 8.6 %collective-permute-start.9 = (f32[16,256]{1,0:T(8,128)S(1)}, f32[16,256]{1,0:T(8,128)S(1)}, u32[]{:S(2)}, u32[]{:S(2)}) collective-permute-start(f32[16,256]{1,0:T(8,128)S(1)} %reduce_sum.9), channel_id=1, source_target_pairs={{32,36},{33,100},{34,164},{35,228},{36,292},{37,356},{38,420},{39,... | collective-permute-start | bytes 49160 | tf_op jit(solution)/shard_map/ppermute | solution.py:265
